TPU v7x, 32 devices: a whole 2x2x4 slice. The times are simulated.
32 devices in a mesh: grp: 2 (over x), dev: 16 (over z, y, core).
Axes of the slice: x: 2, y: 2, z: 4, core: 2. Of those that a mesh axis runs over, the one named last changes fastest.
Arguments:
- inputs: bfloat16 [64, 196, 1024], P(('grp', 'dev')), may hold values from -6 to 6
- cotangent: bfloat16 [64, 196, 1024], P(('grp', 'dev')), may hold values from -6 to 6
- first_gain: float32 [1024], replicated, may hold values from 0.5 to 1.5
- first_shift: float32 [1024], replicated, may hold values from -3 to 3
- token_in: bfloat16 [512, 196], replicated, may hold values from -0.4375 to 0.4375
- token_in_bias: float32 [512], replicated, may hold values from -3 to 3
- token_out: bfloat16 [512, 196], replicated, may hold values from -0.25 to 0.25
- second_gain: float32 [1024], replicated, may hold values from 0.5 to 1.5
- second_shift: float32 [1024], replicated, may hold values from -3 to 3
- channel_in: bfloat16 [1024, 4096], replicated, may hold values from -0.1875 to 0.1875
- channel_in_bias: float32 [4096], replicated, may hold values from -3 to 3
- channel_out: bfloat16 [1024, 4096], replicated, may hold values from -0.09375 to 0.09375
Outputs:
- grad_inputs: bfloat16 [64, 196, 1024], P(('grp', 'dev'))
- grad_token_in: float32 [512, 196], P('dev')
- grad_token_out: float32 [512, 196], P('dev')
- grad_channel_in: float32 [1024, 4096], P('dev')
- grad_channel_out: float32 [1024, 4096], P('dev')
- grad_norms: float32 [5, 1024], replicated
- grad_token_in_bias: float32 [512], replicated
- grad_token_out_bias: float32 [196], replicated
- grad_channel_in_bias: float32 [4096], replicated
All inputs are finite; a program needn't handle non-finite values.
Results may differ from a plain program's by a relative error of at most 0.0066.
Values sent between devices are 32-bit elements; how exact they have to be, the bound alone decides.
A program may use at most 192 MiB of HBM per device.

v0:
```python
import math
import jax
import jax.numpy as jnp
from jax import lax
from jax.sharding import PartitionSpec as P

epsilon = 1e-06


def norm_forward(values, gain, shift):
    centred = values - jnp.mean(values, axis=-1, keepdims=True)
    variance = jnp.mean(centred * centred, axis=-1, keepdims=True)
    inv_std = lax.rsqrt(variance + epsilon)
    scaled = centred * inv_std
    return (scaled * gain + shift, scaled, inv_std)


def norm_backward(incoming, scaled, inv_std, gain):
    weighted = incoming * gain
    first_mean = jnp.mean(weighted, axis=-1, keepdims=True)
    second_mean = jnp.mean(weighted * scaled, axis=-1, keepdims=True)
    return inv_std * (weighted - first_mean - scaled * second_mean)


def gelu_value(values):
    return 0.5 * values * (1.0 + lax.erf(values / math.sqrt(2.0)))


def gelu_slope(values):
    return 0.5 * (1.0 + lax.erf(values / math.sqrt(2.0))) + values * jnp.exp(
        -0.5 * values * values
    ) / math.sqrt(2.0 * math.pi)


def per_device(
    inputs,
    cotangent,
    first_gain,
    first_shift,
    token_in,
    token_in_bias,
    token_out,
    second_gain,
    second_shift,
    channel_in,
    channel_in_bias,
    channel_out,
):
    f32 = jnp.float32
    images, patches, channels = inputs.shape
    x_float = inputs.astype(f32)
    g_float = cotangent.astype(f32)
    normed_one, first_hat, first_rstd = norm_forward(x_float, first_gain, first_shift)
    normed1 = normed_one.astype(jnp.bfloat16)
    hidden1 = (
        jnp.einsum("bpc,sp->bcs", normed1, token_in, preferred_element_type=f32) + token_in_bias
    )
    act1 = gelu_value(hidden1).astype(jnp.bfloat16)
    mixed = x_float + jnp.einsum("bcs,sp->bpc", act1, token_out, preferred_element_type=f32)
    normed_two, second_hat, second_rstd = norm_forward(mixed, second_gain, second_shift)
    normed2 = normed_two.astype(jnp.bfloat16).reshape(-1, channels)
    hidden2 = jnp.dot(normed2, channel_in, preferred_element_type=f32) + channel_in_bias
    act2 = gelu_value(hidden2).astype(jnp.bfloat16)
    cot_rows = cotangent.reshape(-1, channels)
    piece = cot_rows
    chout_part = lax.psum_scatter(
        jnp.einsum("tc,tk->ck", piece, act2, preferred_element_type=f32),
        "dev",
        scatter_dimension=0,
        tiled=True,
    )
    dact2 = jnp.dot(cot_rows, channel_out, preferred_element_type=f32)
    dhidden2 = (dact2 * gelu_slope(hidden2)).astype(jnp.bfloat16)
    piece = normed2
    chin_part = lax.psum_scatter(
        jnp.einsum("tc,tk->ck", piece, dhidden2, preferred_element_type=f32),
        "dev",
        scatter_dimension=0,
        tiled=True,
    )
    dnormed2 = jnp.einsum("tk,ck->tc", dhidden2, channel_in, preferred_element_type=f32).reshape(
        images, patches, channels
    )
    dmixed = g_float + norm_backward(dnormed2, second_hat, second_rstd, second_gain)
    dmixed_round = dmixed.astype(jnp.bfloat16)
    dact1 = jnp.einsum("bpc,sp->bcs", dmixed_round, token_out, preferred_element_type=f32)
    dhidden1 = (dact1 * gelu_slope(hidden1)).astype(jnp.bfloat16)
    dnormed1 = jnp.einsum("bcs,sp->bpc", dhidden1, token_in, preferred_element_type=f32)
    grad_inputs = (dmixed + norm_backward(dnormed1, first_hat, first_rstd, first_gain)).astype(
        jnp.bfloat16
    )
    grad_in_piece = jnp.einsum("bcs,bpc->sp", dhidden1, normed1, preferred_element_type=f32)
    grad_out_piece = jnp.einsum("bcs,bpc->sp", act1, dmixed_round, preferred_element_type=f32)
    token_part = lax.psum_scatter(
        jnp.concatenate([grad_in_piece, grad_out_piece], axis=1),
        "dev",
        scatter_dimension=0,
        tiled=True,
    )
    token_part, chin_part, chout_part = lax.psum((token_part, chin_part, chout_part), "grp")
    norms_part = jnp.stack(
        [
            jnp.sum(dnormed1 * first_hat, axis=(0, 1)),
            jnp.sum(dnormed1, axis=(0, 1)),
            jnp.sum(dnormed2 * second_hat, axis=(0, 1)),
            jnp.sum(dnormed2, axis=(0, 1)),
            jnp.sum(g_float, axis=(0, 1)),
        ]
    )
    tb_in = jnp.sum(dhidden1.astype(f32), axis=(0, 1))
    tb_out = jnp.sum(dmixed, axis=(0, 2))
    cb_in = jnp.sum(dhidden2.astype(f32), axis=0)
    norms_total, tb_in_total, tb_out_total, cb_in_total = lax.psum(
        (norms_part, tb_in, tb_out, cb_in), ("grp", "dev")
    )
    return (
        grad_inputs,
        token_part[:, :patches],
        token_part[:, patches:],
        chin_part,
        chout_part,
        norms_total,
        tb_in_total,
        tb_out_total,
        cb_in_total,
    )


def solution(mesh):
    in_specs = (
        P(("grp", "dev"), None, None),
        P(("grp", "dev"), None, None),
        P(),
        P(),
        P(),
        P(),
        P(),
        P(),
        P(),
        P(),
        P(),
        P(),
    )
    out_specs = (
        P(("grp", "dev"), None, None),
        P("dev", None),
        P("dev", None),
        P("dev", None),
        P("dev", None),
        P(),
        P(),
        P(),
        P(),
    )
    return jax.shard_map(
        per_device, mesh=mesh, in_specs=in_specs, out_specs=out_specs, check_vma=False
    )
```

profile of v0, /device:TPU:0, one launch (start us, length us, event | category | flops | bytes accessed | tf_op | source)
XLA Modules:
  0.0 573.7 jit_solution(3581374591141366518)
XLA Ops:
  7.2 0.0 copy-start
  7.2 0.0 reduce-scatter.12.cloned.1.call-start
  7.2 1.5 convert_reduce_fusion.2
  8.7 1.5 fusion.28
  10.3 0.0 copy-start.3
  10.3 4.7 multiply_convert_fusion.1
  15.0 0.0 copy-start.16
  15.0 1.0 fusion.46
  16.0 0.3 copy-done.5
  16.3 0.3 multiply_reduce_fusion.2
  16.7 0.3 add_convert_fusion
  17.0 1.0 reshape.80
  18.1 0.2 copy.34
  18.3 0.2 reshape.79
  18.4 0.0 copy-start.11
  18.4 0.0 copy-start.18
  18.5 6.4 %fusion.47 = f32[392,4096]{1,0:T(8,128)S(1)} fusion(bf16[392,1024]{1,0:T(8,128)(2,1)} %reshape.80, bf16[1024,4096]{1,0:T(8,128)(2,1)} %param.21), kind=kOutput, calls=%fused_computation.77 | convolution fusion | flops 3288334336 | bytes 15613952 | tf_op jit(solution)/shard_map/dot_general | solution.py:62
  24.9 2.6 copy-done.21
  27.5 8.2 %convolution_bitcast_fusion = f32[1024,4096]{0,1:T(8,128)} fusion(bf16[392,1024]{1,0:T(8,128)(2,1)S(1)} %reshape.79, f32[392,4096]{1,0:T(8,128)S(1)} %fusion.47, f32[4096]{0:T(1024)S(1)} %copy-done.18), kind=kOutput, calls=%fused_computation.1 | convolution fusion | flops 3297968128 | bytes 24018944 | tf_op jit(solution)/shard_map/tc,tk->ck/dot_general | solution.py:67
  35.7 17.5 %copy.43 = f32[1024,4096]{1,0:T(8,128)} copy(f32[1024,4096]{0,1:T(8,128)} %convolution_bitcast_fusion) | data formatting | bytes 33554432
  53.1 0.0 reduce-scatter.12.cloned.1.call-update
  53.2 0.0 copy-start.10
  53.2 0.2 reduce-scatter.8.cloned.1.call-start
  53.4 0.9 copy-done.12
  54.3 8.6 %convert_reduce_fusion = (f32[4096]{0:T(1024)S(1)}, bf16[392,4096]{1,0:T(8,128)(2,1)S(1)}) fusion(f32[392,4096]{1,0:T(8,128)} %copy-done.21, f32[4096]{0:T(1024)S(1)} %copy-done.18, bf16[392,1024]{1,0:T(8,128)(2,1)S(1)} %copy-done.12, bf16[1024,4096]{1,0:T(8,128)(2,1)} %param.23), kind=kOutput, calls=%fused_computation.8 | convolution fusion | flops 3309203456 | bytes 18857984 | tf_op jit(solution)/shard_map/dot_general | solution.py:72
  62.9 1.8 copy-done.24
  64.8 11.0 %fusion.48 = f32[1024,4096]{1,0:T(8,128)} fusion(bf16[392,1024]{1,0:T(8,128)(2,1)S(1)} %copy-done.10, bf16[392,4096]{1,0:T(8,128)(2,1)S(1)} %get-tuple-element.63), kind=kOutput, calls=%fused_computation.78 | convolution fusion | flops 3288334336 | bytes 20791296 | tf_op jit(solution)/shard_map/tc,tk->ck/dot_general | solution.py:76
  75.7 0.0 reduce-scatter.8.cloned.1.call-update
  75.8 0.0 reduce-scatter.10.cloned.1.call-start
  75.8 11.2 %fusion.43 = (f32[1024]{0:T(1024)S(1)}, f32[392]{0:T(512)S(1)}, f32[392,1024]{1,0:T(8,128)}) fusion(f32[1024]{0:T(1024)S(1)} %copy-done.15, bf16[392,4096]{1,0:T(8,128)(2,1)} %copy-done.24, bf16[1024,4096]{1,0:T(8,128)(2,1)} %param.21), kind=kOutput, calls=%fused_computation.73 | convolution fusion | flops 3289537024 | bytes 13215264 | tf_op jit(solution)/shard_map/tk,ck->tc/dot_general | solution.py:81
  87.0 1.6 reshape.81
  88.6 0.1 div.55
  88.6 0.6 multiply_reduce_fusion
  89.3 0.5 copy-done.8
  89.8 0.9 fusion.44
  90.7 0.0 copy-start.14
  90.8 0.6 copy-done.6
  91.4 0.6 convolution_bitcast_fusion.1
  92.0 1.3 copy-done.22
  93.3 0.2 copy-done.14
  93.5 2.4 convert_reduce_fusion.1
  95.9 0.7 convolution_bitcast_fusion.2
  96.6 0.6 copy-done.23
  97.2 0.1 pad_maximum_fusion
  97.3 1.3 copy.41
  98.6 0.0 reduce-scatter.10.cloned.1.call-update
  98.6 0.0 all-reduce.4.cloned.1.call-start
  98.6 134.7 %reduce-scatter.12.cloned.1.call-done = f32[64,4096]{1,0:T(8,128)} async-done(((f32[1024,4096]{1,0:T(8,128)}), f32[64,4096]{1,0:T(8,128)}) %reduce-scatter.12.cloned.1.call-update) | async-done | bytes 1048592
  233.4 3.2 copy.44
  236.6 177.4 %reduce-scatter.8.cloned.1.call-done = f32[64,4096]{1,0:T(8,128)} async-done(((f32[1024,4096]{1,0:T(8,128)}), f32[64,4096]{1,0:T(8,128)}) %reduce-scatter.8.cloned.1.call-update) | async-done | bytes 1048592 | tf_op jit(solution)/shard_map/reduce_scatter | solution.py:75
  413.9 0.0 all-reduce.4.cloned.1.call-update
  414.0 2.8 fusion.27
  416.8 0.6 fusion.26
  417.5 1.7 copy.37
  419.2 0.1 reduce_sum.153
  419.3 40.5 %all-reduce = (f32[5,1024]{1,0:T(8,128)}, f32[512]{0:T(512)}, f32[196]{0:T(256)}, f32[4096]{0:T(1024)}) all-reduce(f32[5,1024]{1,0:T(8,128)S(1)} %stack.23, f32[512]{0:T(512)S(1)} %get-tuple-element.60, f32[196]{0:T(256)S(1)} %get-tuple-element.49, f32[4096]{0:T(1024)S(1)} %get-tuple-element.62), channel_id=1, replica_groups=mesh['grp'=2,'dev'=16] {'grp','dev'}, use_global_device_ids=true, to_apply=%region_19.0 | all-reduce | flops 9924 | bytes 79392 | tf_op jit(solution)/shard_map/psum | solution.py:113
  459.8 15.0 %reduce-scatter.10.cloned.1.call-done = f32[32,392]{1,0:T(8,128)} async-done(((f32[512,392]{1,0:T(8,128)}), f32[32,392]{1,0:T(8,128)}) %reduce-scatter.10.cloned.1.call-update) | async-done | bytes 50192
  474.8 1.0 copy.42
  475.8 13.4 %psum.49 = f32[32,392]{0,1:T(8,128)S(1)} all-reduce(f32[32,392]{0,1:T(8,128)S(1)} %copy.42), channel_id=1, replica_groups=mesh['grp'=2,'dev'=16] {'grp'}, use_global_device_ids=true, to_apply=%region_9.0 | all-reduce | flops 12544 | bytes 100352 | tf_op jit(solution)/shard_map/psum | solution.py:100
  489.3 0.7 copy.38
  489.9 0.7 copy.39
  490.6 72.4 %all-reduce.4.cloned.1.call-done = (f32[64,4096]{1,0:T(8,128)}, f32[64,4096]{0,1:T(8,128)}) async-done(((f32[64,4096]{1,0:T(8,128)}, f32[64,4096]{0,1:T(8,128)}), (f32[64,4096]{1,0:T(8,128)}, f32[64,4096]{0,1:T(8,128)})) %all-reduce.4.cloned.1.call-update) | async-done | bytes 2097168 | tf_op jit(solution)/shard_map/psum | solution.py:100
  563.0 3.2 copy.40
  566.2 1.0 copy.66
  (43 shorter events, 0.2 us)
Async XLA Ops:
  7.2 3.1 copy-start
  7.2 226.2 %reduce-scatter.12.cloned.1.call-start = ((), (), s32[]{:S(2)}) async-start(), calls=%async_computation.5 | async-start | bytes 17825792
  10.3 4.7 copy-start.3
  10.3 4.7 copy-start.13
  15.0 1.3 copy-start.5
  15.0 1.6 copy-start.15
  15.0 1.6 copy-start.16
  16.6 1.4 copy-start.7
  18.4 6.4 %copy-start.11 = (bf16[392,1024]{1,0:T(8,128)(2,1)}, bf16[392,1024]{1,0:T(8,128)(2,1)S(1)}, u32[]{:S(2)}) copy-start(bf16[392,1024]{1,0:T(8,128)(2,1)S(1)} %reshape.79) | copy-start | bytes 2408452
  18.4 9.1 %copy-start.18 = (f32[4096]{0:T(1024)S(1)}, f32[4096]{0:T(1024)}, u32[]{:S(2)}) copy-start(f32[4096]{0:T(1024)} %param.22) | copy-start | bytes 49156
  24.9 2.6 copy-start.21
  53.1 1.1 copy-start.12
  53.2 11.6 %copy-start.10 = (bf16[392,1024]{1,0:T(8,128)(2,1)S(1)}, bf16[392,1024]{1,0:T(8,128)(2,1)}, u32[]{:S(2)}) copy-start(bf16[392,1024]{1,0:T(8,128)(2,1)} %reshape.80) | copy-start | bytes 2408452
  53.2 360.8 %reduce-scatter.8.cloned.1.call-start = ((), (), s32[]{:S(2)}) async-start(), calls=%async_computation.3 | async-start | bytes 17825792 | tf_op jit(solution)/shard_map/reduce_scatter | solution.py:75
  62.9 1.8 copy-start.24
  75.8 399.1 %reduce-scatter.10.cloned.1.call-start = ((), (), s32[]{:S(2)}) async-start(), calls=%async_computation.4 | async-start | bytes 1114112
  88.6 1.1 copy-start.8
  89.8 1.6 copy-start.6
  89.8 3.5 copy-start.22
  90.7 5.1 copy-start.1
  90.7 2.7 copy-start.14
  90.8 2.7 copy-start.20
  93.5 2.4 copy-start.4
  93.5 2.4 copy-start.17
  93.5 2.4 copy-start.19
  95.9 1.3 copy-start.23
  98.6 464.4 %all-reduce.4.cloned.1.call-start = ((), (), s32[]{:S(2)}) async-start(), calls=%async_computation.6 | async-start | bytes 6291456 | tf_op jit(solution)/shard_map/psum | solution.py:100
  414.0 2.9 copy-start.2
  563.0 3.2 copy-start.9
Sparse Core Ops, SparseCore 0:
  53.3 180.0 reduce-scatter.11
  237.5 176.4 reduce-scatter.7
  418.1 56.6 reduce-scatter.9
  477.0 85.9 all-reduce.3
where the time goes:
time: 574 us
  waiting for transfers between devices  400 us (70%)
  matrix products  57.4 us (10%)
  blocking collectives  53.9 us (9%)
  local copies, waits for them, and re-layouts  42.3 us (7%)
  between operations  14.1 us (2%)
  other arithmetic  6.07 us (1%)
    reduce_scatter x1, waiting for transfers between devices, per_device(): lax.psum_scatter(jnp.einsum('tc,tk->ck', piece, dhidden2, preferred_eleme...  177 us
    unnamed x6, waiting for transfers between devices  150 us
    psum x1, waiting for transfers between devices, per_device(): lax.psum((token_part, chin_part, chout_part), 'grp')  72.4 us
    psum x1, blocking collectives, per_device(): lax.psum((norms_part, tb_in, tb_out, cb_in), ('grp', 'dev'))  40.5 us
    unnamed x60, local copies, waits for them, and re-layouts  39.4 us
    psum x1, blocking collectives, per_device(): lax.psum((token_part, chin_part, chout_part), 'grp')  13.4 us
  transfers between devices with their start and end apart: 4, of which 4 were waited for; matrix products, arithmetic and copies ran while one was open for 9% of the time, Pallas kernels for 0%

commit v1 on v0

--- a/solution.py
+++ b/solution.py
@@ -111,7 +111,7 @@
     tb_out = jnp.sum(dmixed, axis=(0, 2))
     cb_in = jnp.sum(dhidden2.astype(f32), axis=0)
     norms_total, tb_in_total, tb_out_total, cb_in_total = lax.psum(
-        (norms_part, tb_in, tb_out, cb_in), ("grp", "dev")
+        lax.psum((norms_part, tb_in, tb_out, cb_in), "dev"), "grp"
     )
     return (
         grad_inputs,

time: 574 us -> 601 us (1.047)
  waiting for transfers between devices: 400 us -> 419 us
  blocking collectives: 53.9 us -> 63.8 us
    psum x1 -> x2, waiting for transfers between devices: 72.4 us -> 108 us  [per_device(): lax.psum((token_part, chin_part, chout_part), 'grp')]
    unnamed x6 -> x7, waiting for transfers between devices: 150 us -> 133 us
    psum x2 -> x1, blocking collectives: 53.9 us -> 63.8 us  [per_device(): lax.psum((norms_part, tb_in, tb_out, cb_in), 'dev')]
    dot_general x1, matrix products: 11.2 us -> 4.76 us  [per_device(): jnp.einsum('tk,ck->tc', dhidden2, channel_in, preferred_element_type=f32)]
    unnamed x60 -> x78, local copies, waits for them, and re-layouts: 39.4 us -> 36.5 us
  transfers between devices with their start and end apart: 4 -> 5, of which waited for: 4 -> 4; matrix products, arithmetic and copies ran while one was open for 9% -> 9% of each run, Pallas kernels for 0% -> 0%
where the time goes in v1:
time: 601 us; the launch traced here: 600 us
  waiting for transfers between devices  419 us (70%)
  blocking collectives  63.8 us (11%)
  matrix products  53.9 us (9%)
  local copies, waits for them, and re-layouts  40.4 us (7%)
  between operations  14.2 us (2%)
  other arithmetic  8.77 us (1%)
    reduce_scatter x1, waiting for transfers between devices, per_device(): lax.psum_scatter(jnp.einsum('tc,tk->ck', piece, dhidden2, preferred_eleme...  177 us
    unnamed x7, waiting for transfers between devices  133 us
    psum x2, waiting for transfers between devices, per_device(): lax.psum((token_part, chin_part, chout_part), 'grp')  108 us
    psum x1, blocking collectives, per_device(): lax.psum((norms_part, tb_in, tb_out, cb_in), 'dev')  63.8 us
    unnamed x78, local copies, waits for them, and re-layouts  36.5 us
  transfers between devices with their start and end apart: 5, of which 4 were waited for; matrix products, arithmetic and copies ran while one was open for 9% of the time, Pallas kernels for 0%

profile of v1, /device:TPU:0, one launch (start us, length us, event | category | flops | bytes accessed | tf_op | source)
XLA Modules:
  0.0 599.9 jit_solution(5412226969463608286)
XLA Ops:
  7.2 0.0 copy-start
  7.2 0.0 reduce-scatter.10.cloned.1.call-start
  7.2 1.5 convert_reduce_fusion.2
  8.7 1.5 fusion.28
  10.3 0.0 copy-start.3
  10.3 4.6 multiply_convert_fusion.1
  15.0 0.0 copy-start.18
  15.0 1.0 fusion.46
  15.9 0.4 copy-done.5
  16.3 0.3 multiply_reduce_fusion.2
  16.6 0.3 add_convert_fusion
  17.0 1.0 reshape.80
  18.0 0.2 copy.34
  18.2 0.2 reshape.79
  18.4 0.0 slice-start
  18.4 6.7 %fusion.47 = f32[392,4096]{1,0:T(8,128)S(1)} fusion(bf16[392,1024]{1,0:T(8,128)(2,1)} %reshape.80, bf16[1024,4096]{1,0:T(8,128)(2,1)} %param.21), kind=kOutput, calls=%fused_computation.77 | convolution fusion | flops 3288334336 | bytes 15613952 | tf_op jit(solution)/shard_map/dot_general | solution.py:62
  25.2 0.0 slice-start.1
  25.2 10.0 %convert_reduce_fusion = (f32[4096]{0:T(1024)S(1)}, bf16[392,4096]{1,0:T(8,128)(2,1)S(1)}) fusion(f32[392,4096]{1,0:T(8,128)S(1)} %fusion.47, f32[4096]{0:T(1024)S(1)} %copy-done.22, bf16[392,1024]{1,0:T(8,128)(2,1)S(1)} %reshape.79, bf16[1024,4096]{1,0:T(8,128)(2,1)} %param.23), kind=kOutput, calls=%fused_computation.8 | convolution fusion | flops 3309203456 | bytes 18857984 | tf_op jit(solution)/shard_map/dot_general | solution.py:72
  35.2 4.8 fusion.43
  40.0 1.6 reshape.81
  41.6 0.6 multiply_reduce_fusion
  42.2 0.1 div.55
  42.3 2.2 fusion.44
  44.6 0.6 convolution_bitcast_fusion.1
  45.2 0.2 copy-done.27
  45.3 0.4 copy-done.14
  45.8 2.4 convert_reduce_fusion.1
  48.2 0.6 convolution_bitcast_fusion.2
  48.8 0.7 copy-done.28
  49.5 0.1 pad_maximum_fusion
  49.6 1.3 copy.41
  50.9 0.0 reduce-scatter.10.cloned.1.call-update
  50.9 0.0 reduce-scatter.12.cloned.1.call-start
  51.0 10.4 %convolution_bitcast_fusion = f32[1024,4096]{0,1:T(8,128)} fusion(bf16[392,1024]{1,0:T(8,128)(2,1)S(1)} %copy-done.12, f32[392,4096]{1,0:T(8,128)} %copy-done.26, f32[4096]{0:T(1024)S(1)} %copy-done.23), kind=kOutput, calls=%fused_computation.1 | convolution fusion | flops 3297968128 | bytes 24018944 | tf_op jit(solution)/shard_map/tc,tk->ck/dot_general | solution.py:67
  61.5 17.6 %copy.43 = f32[1024,4096]{1,0:T(8,128)} copy(f32[1024,4096]{0,1:T(8,128)} %convolution_bitcast_fusion) | data formatting | bytes 33554432
  79.0 0.0 reduce-scatter.12.cloned.1.call-update
  79.1 0.0 reduce-scatter.8.cloned.1.call-start
  79.1 1.1 copy-done.10
  80.2 10.1 %fusion.48 = f32[1024,4096]{1,0:T(8,128)} fusion(bf16[392,1024]{1,0:T(8,128)(2,1)S(1)} %copy-done.10, bf16[392,4096]{1,0:T(8,128)(2,1)} %copy-done.29), kind=kOutput, calls=%fused_computation.78 | convolution fusion | flops 3288334336 | bytes 20791296 | tf_op jit(solution)/shard_map/tc,tk->ck/dot_general | solution.py:76
  90.3 0.0 reduce-scatter.8.cloned.1.call-update
  90.3 0.0 all-reduce.6.cloned.1.call-start
  90.4 2.7 fusion.27
  93.1 0.1 reduce_sum.153
  93.3 63.8 %all-reduce = (f32[5,1024]{1,0:T(8,128)}, f32[512]{0:T(512)}, f32[196]{0:T(256)}, f32[4096]{0:T(1024)}) all-reduce(f32[5,1024]{1,0:T(8,128)S(1)} %stack.23, f32[512]{0:T(512)S(1)} %get-tuple-element.65, f32[196]{0:T(256)S(1)} %get-tuple-element.54, f32[4096]{0:T(1024)S(1)} %get-tuple-element.67), channel_id=1, replica_groups=mesh['grp'=2,'dev'=16] {'dev'}, use_global_device_ids=true, to_apply=%region_19.0 | all-reduce | flops 9924 | bytes 79392 | tf_op jit(solution)/shard_map/psum | solution.py:114
  157.1 1.7 copy.42
  158.8 0.0 all-reduce.6.cloned.1.call-update
  158.8 0.0 all-reduce.8.cloned.1.call-start
  158.9 133.1 %reduce-scatter.12.cloned.1.call-done = f32[64,4096]{1,0:T(8,128)} async-done(((f32[1024,4096]{1,0:T(8,128)}), f32[64,4096]{1,0:T(8,128)}) %reduce-scatter.12.cloned.1.call-update) | async-done | bytes 1048592
  292.0 3.2 copy.44
  295.2 177.4 %reduce-scatter.8.cloned.1.call-done = f32[64,4096]{1,0:T(8,128)} async-done(((f32[1024,4096]{1,0:T(8,128)}), f32[64,4096]{1,0:T(8,128)}) %reduce-scatter.8.cloned.1.call-update) | async-done | bytes 1048592 | tf_op jit(solution)/shard_map/reduce_scatter | solution.py:75
  472.5 0.0 all-reduce.8.cloned.1.call-update
  472.6 2.0 fusion.26
  474.6 1.7 copy.37
  476.3 22.3 %all-reduce.6.cloned.1.call-done = (f32[32,392]{0,1:T(8,128)}, f32[5,1024]{1,0:T(8,128)}, f32[512]{0:T(512)}, f32[196]{0:T(256)}, f32[4096]{0:T(1024)}) async-done(((f32[32,392]{0,1:T(8,128)}, f32[5,1024]{1,0:T(8,128)}, f32[512]{0:T(512)}, f32[196]{0:T(256)}, f32[4096]{0:T(1024)}), (f32[32,392]{0,1:T(8,128)}, f32[5,1024]{1,0:T(8,128)}, f32[512]{0:T(512)}, f32[196]{0:T(256)}, ...) | async-done | bytes 89888 | tf_op jit(solution)/shard_map/psum | solution.py:100
  498.6 1.0 fusion.45
  499.6 0.7 copy.38
  500.3 0.7 copy.39
  501.0 85.8 %all-reduce.8.cloned.1.call-done = (f32[64,4096]{1,0:T(8,128)}, f32[64,4096]{0,1:T(8,128)}) async-done(((f32[64,4096]{1,0:T(8,128)}, f32[64,4096]{0,1:T(8,128)}), (f32[64,4096]{1,0:T(8,128)}, f32[64,4096]{0,1:T(8,128)})) %all-reduce.8.cloned.1.call-update) | async-done | bytes 2097168 | tf_op jit(solution)/shard_map/psum | solution.py:100
  586.8 3.2 copy.40
  590.0 1.0 copy.71
  591.0 0.6 copy.72
  591.6 0.6 copy.73
  592.2 0.6 copy.74
  592.8 0.6 copy.75
  (64 shorter events, 0.2 us)
Async XLA Ops:
  7.2 3.1 copy-start
  7.2 149.9 %reduce-scatter.10.cloned.1.call-start = ((), (), s32[]{:S(2)}) async-start(), calls=%async_computation.4 | async-start | bytes 1114112
  10.3 4.7 copy-start.3
  10.3 4.7 copy-start.13
  14.9 1.4 copy-start.5
  14.9 1.7 copy-start.15
  15.0 1.7 copy-start.18
  16.6 1.4 copy-start.8
  18.4 6.7 %copy-start.11 = (bf16[392,1024]{1,0:T(8,128)(2,1)}, bf16[392,1024]{1,0:T(8,128)(2,1)S(1)}, u32[]{:S(2)}) copy-start(bf16[392,1024]{1,0:T(8,128)(2,1)S(1)} %reshape.79) | copy-start | bytes 2408452
  18.4 6.7 %copy-start.22 = (f32[4096]{0:T(1024)S(1)}, f32[4096]{0:T(1024)}, u32[]{:S(2)}) copy-start(f32[4096]{0:T(1024)} %param.22) | copy-start | bytes 49156
  18.4 16.8 %slice-start = ((s8[8388608]{0:T(1024)(128)(4,1)}), s8[4194304]{0:T(1024)(128)(4,1)S(1)}, s32[]{:S(2)}) async-start(s8[8388608]{0:T(1024)(128)(4,1)} %bitcast.60), calls=%async_computation.8 | async-start | bytes 8388608
  25.2 10.0 %copy-start.26 = (f32[392,4096]{1,0:T(8,128)}, f32[392,4096]{1,0:T(8,128)S(1)}, u32[]{:S(2)}) copy-start(f32[392,4096]{1,0:T(8,128)S(1)} %fusion.47) | copy-start | bytes 19267588
  25.2 10.0 %slice-start.1 = ((s8[8388608]{0:T(1024)(128)(4,1)}), s8[4194304]{0:T(1024)(128)(4,1)S(1)}, s32[]{:S(2)}) async-start(s8[8388608]{0:T(1024)(128)(4,1)} %bitcast.60), calls=%async_computation.9 | async-start | bytes 8388608
  35.2 4.8 copy-start.29
  42.3 2.3 copy-start.6
  42.3 3.1 copy-start.27
  44.5 3.6 copy-start.1
  44.5 1.3 copy-start.14
  44.5 1.2 copy-start.25
  45.8 2.4 copy-start.4
  45.8 2.4 copy-start.19
  45.8 2.4 copy-start.24
  48.2 1.4 copy-start.28
  49.5 1.5 copy-start.12
  49.5 1.5 copy-start.23
  50.9 241.0 %reduce-scatter.12.cloned.1.call-start = ((), (), s32[]{:S(2)}) async-start(), calls=%async_computation.5 | async-start | bytes 17825792
  79.0 1.1 copy-start.10
  79.1 393.4 %reduce-scatter.8.cloned.1.call-start = ((), (), s32[]{:S(2)}) async-start(), calls=%async_computation.3 | async-start | bytes 17825792 | tf_op jit(solution)/shard_map/reduce_scatter | solution.py:75
  90.3 408.3 %all-reduce.6.cloned.1.call-start = ((), (), s32[]{:S(2)}) async-start(), calls=%async_computation.6 | async-start | bytes 505856 | tf_op jit(solution)/shard_map/psum | solution.py:100
  93.1 198.8 %copy-start.7 = (f32[2,1024,196]{1,2,0:T(8,128)}, f32[2,1024,196]{1,2,0:T(8,128)S(1)}, u32[]{:S(2)}) copy-start(f32[2,1024,196]{1,2,0:T(8,128)S(1)} %get-tuple-element.64) | copy-start | bytes 4816900
  158.8 428.0 %all-reduce.8.cloned.1.call-start = ((), (), s32[]{:S(2)}) async-start(), calls=%async_computation.7 | async-start | bytes 6291456 | tf_op jit(solution)/shard_map/psum | solution.py:100
  295.2 177.4 %copy-start.2 = (f32[2,196,1024]{2,1,0:T(8,128)S(1)}, f32[2,196,1024]{2,1,0:T(8,128)}, u32[]{:S(2)}) copy-start(f32[2,196,1024]{2,1,0:T(8,128)} %copy-done.1) | copy-start | bytes 4816900
  586.8 3.3 copy-start.9
  586.8 4.2 copy-start.16
  586.8 4.8 copy-start.20
  586.8 5.4 copy-start.21
  586.8 6.0 copy-start.17
Sparse Core Ops, SparseCore 0:
  51.1 60.3 reduce-scatter.9
  115.6 176.3 reduce-scatter.11
  296.1 176.3 reduce-scatter.7
  476.0 22.5 all-reduce.5
  500.8 85.9 all-reduce.7
